TPU v7x, 32 devices: a whole 2x2x4 slice. The times are simulated.
32 devices in a mesh: row: 4 (over z), col: 8 (over y, x, core).
Axes of the slice: x: 2, y: 2, z: 4, core: 2. Of those that a mesh axis runs over, the one named last changes fastest.
Arguments:
- response_coeffs: float32 [3, 8192, 1024], P(None, ('row', 'col')), may hold values from -6 to 6
- occupied_coeffs: float32 [8192, 1024], P(('row', 'col')), may hold values from -0.1875 to 0.1875
Outputs:
- density: float32 [3, 8192, 8192], P(None, 'row', 'col')
All inputs are finite; a program needn't handle non-finite values.
Results may differ from a plain program's by a relative error of at most 0.0003.
Values sent between devices are 32-bit elements; how exact they have to be, the bound alone decides.
A program may use at most 256 MiB of HBM per device.

v0:
```python
import jax
import jax.numpy as jnp
from jax import lax
from jax.sharding import PartitionSpec as P

SLICE_PAIRS = ((0, 0), (0, 1), (1, 0))


def partner(value, axis, stride):
    mask = 2**stride
    pairs = [(source, source ^ mask) for source in range(lax.axis_size(axis))]
    return lax.ppermute(value, axis, pairs)


def split_slices(values):
    leading = lax.optimization_barrier(values.astype(jnp.bfloat16))
    remainder = values - leading.astype(jnp.float32)
    trailing = lax.optimization_barrier(remainder.astype(jnp.bfloat16))
    return [leading, trailing]


def contribute(row_slices, column_slices, perturbations):
    accumulated = jnp.zeros(
        (perturbations, row_slices[0].shape[1], column_slices[0].shape[1]), jnp.float32
    )
    for left_index, right_index in SLICE_PAIRS:
        forward_term = jnp.einsum(
            "kro,co->krc",
            row_slices[left_index][:perturbations],
            column_slices[right_index][perturbations],
            preferred_element_type=jnp.float32,
        )
        mirror_term = jnp.einsum(
            "ro,kco->krc",
            row_slices[right_index][perturbations],
            column_slices[left_index][:perturbations],
            preferred_element_type=jnp.float32,
        )
        accumulated = accumulated + forward_term + mirror_term
    return accumulated


def relay_columns(stacked, perturbations):
    rows_total = lax.axis_size("row")
    columns_total = lax.axis_size("col")
    col_index = lax.axis_index("col")
    shard_rows = stacked.shape[1]
    orbitals = stacked.shape[2]
    half_rows = shard_rows // 2
    swap_bit = rows_total.bit_length() - 1
    own_first = stacked[:, :half_rows]
    partner_second = partner(stacked[:, half_rows:], "col", swap_bit)
    even_first = col_index // rows_total == 0
    leading = jnp.where(even_first, own_first, partner_second)
    trailing = jnp.where(even_first, partner_second, own_first)
    paired = jnp.concatenate([leading, trailing], axis=1)
    gathered = lax.all_gather(paired, "row", axis=1, tiled=True)
    regrouped = lax.all_to_all(gathered, "col", split_axis=1, concat_axis=1, tiled=True)
    shaped = regrouped.reshape(perturbations + 1, 2, rows_total, half_rows, orbitals)
    flipped = shaped[:, ::-1]
    ordered = jnp.where(col_index % 2 == 0, shaped, flipped)
    return jnp.swapaxes(ordered, 1, 2).reshape(
        perturbations + 1, columns_total * half_rows, orbitals
    )


def shards(response_coeffs, occupied_coeffs):
    perturbations = response_coeffs.shape[0]
    stacked = jnp.concatenate([response_coeffs, occupied_coeffs[None]], axis=0)
    column_panel = relay_columns(stacked, perturbations)
    column_slices = split_slices(column_panel)
    return contribute(
        split_slices(lax.all_gather(stacked, "col", axis=1, tiled=True)),
        column_slices,
        perturbations,
    )


def solution(mesh):
    return jax.shard_map(
        shards,
        mesh=mesh,
        in_specs=(P(None, ("row", "col"), None), P(("row", "col"), None)),
        out_specs=P(None, "row", "col"),
        check_vma=False,
    )
```

profile of v0, /device:TPU:0, one launch (start us, length us, event | category | flops | bytes accessed | tf_op | source)
XLA Modules:
  0.0 913.4 jit_solution(8449333909172042322)
XLA Ops:
  6.5 3.2 fusion.7
  9.8 3.0 collective-permute-start
  12.8 45.9 %collective-permute-done = f32[4,128,1024]{2,1,0:T(8,128)} collective-permute-done((f32[4,128,1024]{2,1,0:T(8,128)}, f32[4,128,1024]{2,1,0:T(8,128)}, u32[]{:S(2)}, u32[]{:S(2)}) %collective-permute-start) | collective-permute-done | bytes 2097184 | tf_op jit(solution)/shard_map/ppermute | solution.py:12
  58.7 2.4 broadcast_select_fusion.1
  61.1 2.5 pad_maximum_fusion.1
  63.7 3.7 pad_maximum_fusion
  67.4 284.7 %all-gather.5.cloned.1.call-done = f32[4,1024,1024]{2,1,0:T(8,128)} async-done(((f32[4,256,1024]{2,1,0:T(8,128)}), f32[4,1024,1024]{2,1,0:T(8,128)}) %all-gather.5.cloned.1.call-update) | async-done | bytes 16777232 | tf_op jit(solution)/shard_map/all_gather | solution.py:57
  352.1 21.6 %copy.8 = f32[4,1024,1024]{2,0,1:T(4,128)} copy(f32[4,1024,1024]{2,1,0:T(8,128)} %all-gather.5.cloned.1.call-done) | data formatting | bytes 33554432 | tf_op jit(solution)/shard_map/all_gather | solution.py:57
  373.7 6.0 all-to-all-start
  379.7 302.3 %all-to-all-done = f32[4,1024,1024]{2,0,1:T(4,128)} async-done(((f32[4,1024,1024]{2,0,1:T(4,128)}), f32[4,1024,1024]{2,0,1:T(4,128)}, u32[]{:S(2)}, u32[]{:S(2)}) %all-to-all-start) | async-done | bytes 16777248 | tf_op jit(solution)/shard_map/all_to_all | solution.py:58
  682.0 15.2 %copy.10 = f32[4,2,4,128,1024]{4,3,1,2,0:T(8,128)S(1)} copy(f32[4,2,4,128,1024]{4,0,3,2,1:T(4,128)} %bitcast.1) | data formatting | bytes 33554432 | tf_op jit(solution)/shard_map/reshape | solution.py:59
  697.2 3.4 reverse_select_fusion
  700.6 2.4 bitcast_convert_fusion
  703.1 3.2 copy-done.1
  706.3 6.3 fusion.2
  712.6 12.1 %convert_element_type.18 = bf16[4,2048,1024]{2,1,0:T(8,128)(2,1)S(1)} convert(f32[4,2048,1024]{2,1,0:T(8,128)} %all-gather.3.cloned.1.call-done) | non-fusion elementwise | flops 8388608 | bytes 50331648 | tf_op jit(solution)/shard_map/convert_element_type | solution.py:16
  724.7 5.8 copy-done
  730.5 19.0 %fusion.4 = f32[3,1024,2048]{1,2,0:T(8,128)} fusion(bf16[4,1024,1024]{2,1,0:T(8,128)(2,1)} %fusion.2, bf16[4,2048,1024]{2,1,0:T(8,128)(2,1)S(1)} %convert_element_type.18), kind=kOutput, calls=%fused_computation.19 | convolution fusion | flops 12884901888 | bytes 37748736 | tf_op jit(solution)/shard_map/ro,kco->krc/dot_general | solution.py:33
  749.5 22.0 %fusion.8 = f32[3,2048,1024]{2,1,0:T(8,128)} fusion(bf16[4,2048,1024]{2,1,0:T(8,128)(2,1)} %copy-done, bf16[4,1024,1024]{2,1,0:T(8,128)(2,1)} %fusion.2), kind=kOutput, calls=%fused_computation.24 | convolution fusion | flops 12884901888 | bytes 44040192 | tf_op jit(solution)/shard_map/kro,co->krc/dot_general | solution.py:27
  771.5 21.8 %fusion.9 = f32[3,2048,1024]{2,1,0:T(8,128)} fusion(bf16[4,2048,1024]{2,1,0:T(8,128)(2,1)} %copy-done, bf16[4,1024,1024]{2,1,0:T(8,128)(2,1)} %copy-done.1), kind=kOutput, calls=%fused_computation.26 | convolution fusion | flops 12884901888 | bytes 44040192 | tf_op jit(solution)/shard_map/kro,co->krc/dot_general | solution.py:27
  793.3 20.0 %fusion.5 = f32[3,1024,2048]{1,2,0:T(8,128)} fusion(bf16[4,1024,1024]{2,1,0:T(8,128)(2,1)} %copy-done.1, bf16[4,2048,1024]{2,1,0:T(8,128)(2,1)} %copy-done), kind=kOutput, calls=%fused_computation.20 | convolution fusion | flops 12884901888 | bytes 37748736 | tf_op jit(solution)/shard_map/ro,kco->krc/dot_general | solution.py:33
  813.3 19.5 %subtract_convert_fusion = bf16[4,2048,1024]{2,1,0:T(8,128)(2,1)} fusion(f32[4,2048,1024]{2,1,0:T(8,128)} %all-gather.3.cloned.1.call-done, bf16[4,2048,1024]{2,1,0:T(8,128)(2,1)S(1)} %bitcast.54), kind=kLoop, calls=%fused_computation | loop fusion | flops 25165824 | bytes 67108864 | tf_op jit(solution)/shard_map/convert_element_type | solution.py:18
  832.8 20.0 %fusion.3 = f32[3,1024,2048]{1,2,0:T(8,128)} fusion(bf16[4,1024,1024]{2,1,0:T(8,128)(2,1)} %copy-done.1, bf16[4,2048,1024]{2,1,0:T(8,128)(2,1)} %subtract_convert_fusion), kind=kOutput, calls=%fused_computation.16 | convolution fusion | flops 12884901888 | bytes 37748736 | tf_op jit(solution)/shard_map/ro,kco->krc/dot_general | solution.py:33
  852.8 53.5 %bitcast_add_fusion = f32[3,2048,1024]{2,1,0:T(8,128)} fusion(f32[3,1024,2048]{1,2,0:T(8,128)} %fusion.4, f32[3,1024,2048]{1,2,0:T(8,128)} %fusion.3, f32[3,2048,1024]{2,1,0:T(8,128)} %fusion.8, f32[3,2048,1024]{2,1,0:T(8,128)} %fusion.9, f32[3,1024,2048]{1,2,0:T(8,128)} %fusion.5, bf16[4,2048,1024]{2,1,0:T(8,128)(2,1)} %subtract_convert_fusion, ...), kind=kOutput, calls=%fused_computation.1 | convolution fusion | flops 12916359168 | bytes 169869312 | tf_op jit(solution)/shard_map/kro,co->krc/dot_general | solution.py:27
  (18 shorter events, 0.1 us)
Async XLA Ops:
  6.5 52.2 %copy-start.2 = (f32[3,256,1024]{2,1,0:T(8,128)S(1)}, f32[3,256,1024]{2,1,0:T(8,128)}, u32[]{:S(2)}) copy-start(f32[3,256,1024]{2,1,0:T(8,128)} %param.2) | copy-start | bytes 9437188
  6.5 345.5 %all-gather.5.cloned.1.call-start = ((), (), s32[]{:S(2)}) async-start(), calls=%async_computation.2 | async-start | bytes 20971520 | tf_op jit(solution)/shard_map/all_gather | solution.py:57
  9.8 48.9 %collective-permute-start = (f32[4,128,1024]{2,1,0:T(8,128)}, f32[4,128,1024]{2,1,0:T(8,128)}, u32[]{:S(2)}, u32[]{:S(2)}) collective-permute-start(f32[4,128,1024]{2,1,0:T(8,128)} %fusion.7), channel_id=1, source_target_pairs={{0,4},{1,5},{2,6},{3,7},{4,0},{5,1},{6,2},{7,3},{8,12},{9,13},{10,... | collective-permute-start | bytes 6291464 | tf_op jit(solution)/shard_map/ppermute | solution.py:12
  63.7 648.9 %all-gather.3.cloned.1.call-start = ((), (), s32[]{:S(2)}) async-start(), calls=%async_computation.1 | async-start | bytes 37748736 | tf_op jit(solution)/shard_map/all_gather | solution.py:73
  373.7 308.3 %all-to-all-start = ((f32[4,1024,1024]{2,0,1:T(4,128)}), f32[4,1024,1024]{2,0,1:T(4,128)}, u32[]{:S(2)}, u32[]{:S(2)}) async-start(f32[4,1024,1024]{2,0,1:T(4,128)} %copy.8), calls=%async_computation | async-start | bytes 33554432 | tf_op jit(solution)/shard_map/all_to_all | solution.py:58
  703.1 3.2 copy-start.1
  724.7 5.8 copy-start
  771.5 41.8 %slice-start = ((s8[16777216]{0:T(1024)(128)(4,1)}), s8[4194304]{0:T(1024)(128)(4,1)S(1)}, s32[]{:S(2)}) async-start(s8[16777216]{0:T(1024)(128)(4,1)} %bitcast.53), calls=%async_computation.3 | async-start | bytes 8388608
  771.5 41.8 %slice-start.1 = ((s8[16777216]{0:T(1024)(128)(4,1)}), s8[4194304]{0:T(1024)(128)(4,1)S(1)}, s32[]{:S(2)}) async-start(s8[16777216]{0:T(1024)(128)(4,1)} %bitcast.53), calls=%async_computation.4 | async-start | bytes 8388608
  793.3 20.0 %slice-start.2 = ((s8[16777216]{0:T(1024)(128)(4,1)}), s8[4194304]{0:T(1024)(128)(4,1)S(1)}, s32[]{:S(2)}) async-start(s8[16777216]{0:T(1024)(128)(4,1)} %bitcast.53), calls=%async_computation.5 | async-start | bytes 8388608
  793.3 20.0 %slice-start.3 = ((s8[16777216]{0:T(1024)(128)(4,1)}), s8[4194304]{0:T(1024)(128)(4,1)S(1)}, s32[]{:S(2)}) async-start(s8[16777216]{0:T(1024)(128)(4,1)} %bitcast.53), calls=%async_computation.6 | async-start | bytes 8388608
Sparse Core Ops, SparseCore 0:
  63.8 288.2 all-gather.4
  353.9 325.4 all-gather.2
where the time goes:
time: 918 us; the launch traced here: 913 us
  waiting for transfers between devices  633 us (69%)
  matrix products  156 us (17%)
  other arithmetic  55.5 us (6%)
  local copies, waits for them, and re-layouts  45.9 us (5%)
  between operations  13.7 us (1%)
    all_to_all x1, waiting for transfers between devices, relay_columns(): lax.all_to_all(gathered, 'col', split_axis=1, concat_axis=1, tiled=True)  302 us
    all_gather x1, waiting for transfers between devices, relay_columns(): gathered = lax.all_gather(paired, 'row', axis=1, tiled=True)  285 us
    dot_general x3, matrix products, contribute(): jnp.einsum('kro,co->krc', row_slices[left_index][:perturbations], column_...  97.3 us
    dot_general x3, matrix products, contribute(): jnp.einsum('ro,kco->krc', row_slices[right_index][perturbations], column_...  59 us
    ppermute x1, waiting for transfers between devices, partner(): return lax.ppermute(value, axis, pairs)  45.9 us
    convert_element_type x2, other arithmetic, split_slices(): trailing = lax.optimization_barrier(remainder.astype(jnp.bfloat16))  25.8 us
    all_gather x1, local copies, waits for them, and re-layouts, relay_columns(): gathered = lax.all_gather(paired, 'row', axis=1, tiled=True)  21.6 us
  transfers between devices with their start and end apart: 4, of which 3 were waited for; matrix products, arithmetic and copies ran while one was open for 6% of the time, Pallas kernels for 0%

commit v1 on v0

--- a/solution.py
+++ b/solution.py
@@ -1,6 +1,10 @@
+import functools
+
 import jax
 import jax.numpy as jnp
 from jax import lax
+from jax.experimental import pallas as pl
+from jax.experimental.pallas import tpu as pltpu
 from jax.sharding import PartitionSpec as P
 
 SLICE_PAIRS = ((0, 0), (0, 1), (1, 0))
@@ -76,9 +80,313 @@
     )
 
 
+HALVES = 2
+
+
+def flip(value):
+    return value + 1 - 2 * (value % 2)
+
+
+def across(value):
+    return value + 2 - 4 * (value // 2)
+
+
+def panel_kernel(
+    resp, occ, out, rowbuf, colbuf,
+    row_lead, row_trail, col_lead, col_trail, stage, tile,
+    rx_row, rx_col, tx, stage_sem, tile_sem,
+):
+    perturbations, shard_rows, orbitals = resp.shape
+    kinds = perturbations + 1
+    piece = shard_rows // HALVES
+    pieces = kinds * HALVES
+    early = pieces // 2
+    positions = 4 * pieces
+    block_rows = tile.shape[2]
+    row_blocks = 8 * shard_rows // block_rows
+    panel_rows = 8 * shard_rows
+
+    z = lax.axis_index("row")
+    planes = lax.axis_size("row")
+    column = lax.axis_index("col")
+    w, core = column // 2, column % 2
+    xq, yq, dq = flip(w), across(w), flip(across(w))
+    other = 1 - core
+    x_dev, y_dev, p_dev = (z, 2 * xq + core), (z, 2 * yq + core), (z, 2 * w + other)
+    up_dev, down_dev = (z + 1, column), (z - 1, column)
+    has_up, has_down = z < planes - 1, z > 0
+    diagonal = z == w
+    match = w // 2 == core
+    distance = jnp.where(z > w, z - w, w - z)
+
+    barrier = pltpu.get_barrier_semaphore()
+
+    def greet(device):
+        pl.semaphore_signal(barrier, inc=1, device_id=device, device_id_type=pl.DeviceIdType.MESH)
+
+    above, below = (z + 1) % planes, (z + planes - 1) % planes
+    for device in (x_dev, y_dev, p_dev, (above, column), (below, column)):
+        greet(device)
+    pl.semaphore_wait(barrier, 5)
+
+    def row_piece(quarter, lane, j):
+        return rowbuf.at[2 * quarter + lane, j // HALVES, pl.ds(pl.multiple_of((j % HALVES) * piece, piece), piece)]
+
+    def col_piece(p):
+        i, j = p // pieces, p % pieces
+        return colbuf.at[i, j // HALVES, pl.ds(pl.multiple_of((j % HALVES) * piece, piece), piece)]
+
+    def send(source, target, send_sem, recv_sem, device):
+        pltpu.make_async_remote_copy(
+            src_ref=source, dst_ref=target, send_sem=send_sem, recv_sem=recv_sem,
+            device_id=device, device_id_type=pl.DeviceIdType.MESH,
+        ).start()
+
+    def send_row(quarter, lane, j, slot, device):
+        ref = row_piece(quarter, lane, j)
+        send(ref, ref, tx.at[slot], rx_row.at[2 * quarter + lane, j], device)
+
+    def wait_row(quarter, lane, j):
+        ref = row_piece(quarter, lane, j)
+        pltpu.make_async_copy(ref, ref, rx_row.at[2 * quarter + lane, j]).wait()
+
+    load_resp = pltpu.make_async_copy(resp, stage.at[pl.ds(0, perturbations)], stage_sem.at[0])
+    load_occ = pltpu.make_async_copy(occ, stage.at[perturbations], stage_sem.at[1])
+    load_resp.start()
+    load_occ.start()
+    for j in range(pieces):
+        k, rows = j // HALVES, pl.ds((j % HALVES) * piece, piece)
+        source = resp.at[k, rows] if k < perturbations else occ.at[rows]
+        for slot, device in ((0, x_dev), (1, y_dev), (4, p_dev)):
+            send(source, row_piece(w, core, j), tx.at[slot], rx_row.at[2 * w + core, j], device)
+    load_resp.wait()
+    load_occ.wait()
+    keep = pltpu.make_async_copy(stage, rowbuf.at[2 * w + core], stage_sem.at[0])
+    keep.start()
+    keep.wait()
+
+    first = jnp.where(match, w, yq)
+    second = flip(first)
+
+    def order(i):
+        quarter = jnp.where(i < 2, first, second)
+        lane = jnp.where(i % 2 == 0, core, other)
+        return quarter, lane
+
+    def emit(source, p):
+        @pl.when(has_up & (z >= w))
+        def _():
+            send(source, col_piece(p), tx.at[5], rx_col.at[p], up_dev)
+
+        @pl.when(has_down & (z <= w))
+        def _():
+            send(source, col_piece(p), tx.at[6], rx_col.at[p], down_dev)
+
+    def emit_own(p):
+        quarter, lane = order(p // pieces)
+        emit(row_piece(quarter, lane, p % pieces), p)
+
+    def split_into(value, lead, trail, start):
+        leading = value.astype(jnp.bfloat16)
+        lead[pl.ds(start, shard_rows), :] = leading
+        trail[pl.ds(start, shard_rows), :] = (value - leading.astype(jnp.float32)).astype(jnp.bfloat16)
+
+    def load_stage(source):
+        copy = pltpu.make_async_copy(source, stage, stage_sem.at[0])
+        copy.start()
+        copy.wait()
+
+    def tile_copy(slot, block, start):
+        return pltpu.make_async_copy(
+            tile.at[slot],
+            out.at[:, pl.ds(pl.multiple_of(block * block_rows, block_rows), block_rows),
+                   pl.ds(pl.multiple_of(start, shard_rows), shard_rows)],
+            tile_sem.at[slot],
+        )
+
+    gathered = pieces + early
+    convert_at = gathered + 1
+    matmul_at = convert_at + 8
+    rounds = positions + planes - 1
+    hidden = 3 * row_blocks
+    tasks = 4 * row_blocks
+
+    def step(t, carry):
+        @pl.when(t < pieces)
+        def _():
+            wait_row(xq, core, t)
+            send_row(xq, core, t, 4, p_dev)
+            wait_row(yq, core, t)
+            send_row(yq, core, t, 4, p_dev)
+            wait_row(w, other, t)
+
+            @pl.when(t < early)
+            def _():
+                send_row(yq, core, t, 2, x_dev)
+
+            @pl.when(t >= early)
+            def _():
+                send_row(xq, core, t, 3, y_dev)
+
+        @pl.when((t >= 1) & (t < pieces + 1))
+        def _():
+            wait_row(xq, other, t - 1)
+            wait_row(yq, other, t - 1)
+
+        @pl.when((t >= pieces) & (t < gathered))
+        def _():
+            for shift in (0, early):
+                wait_row(dq, core, t - pieces + shift)
+                send_row(dq, core, t - pieces + shift, 4, p_dev)
+
+        @pl.when((t >= pieces + 1) & (t < gathered + 1))
+        def _():
+            for shift in (0, early):
+                wait_row(dq, other, t - pieces - 1 + shift)
+
+        @pl.when(diagonal & match & (t < positions // 2))
+        def _():
+            emit_own(2 * t)
+            emit_own(2 * t + 1)
+
+        @pl.when(diagonal & (w // 2 != core) & (t < positions))
+        def _():
+            emit_own(t)
+
+        @pl.when((z != w) & (t >= distance) & (t < positions + distance))
+        def _():
+            p = t - distance
+            ref = col_piece(p)
+            pltpu.make_async_copy(ref, ref, rx_col.at[p]).wait()
+            emit(ref, p)
+
+        @pl.when((t >= convert_at) & (t < matmul_at))
+        def _():
+            shard = t - convert_at
+            load_stage(rowbuf.at[shard])
+
+            def convert(k, carry):
+                start = pl.multiple_of(k * panel_rows + shard * shard_rows, shard_rows)
+                split_into(stage[k], row_lead, row_trail, start)
+                return carry
+
+            lax.fori_loop(0, kinds, convert, 0)
+
+        @pl.when(((t >= matmul_at) & (t < matmul_at + hidden)) | (t >= rounds))
+        def _():
+            task = jnp.where(t >= rounds, t - rounds + hidden, t - matmul_at)
+            part, block = task // row_blocks, task % row_blocks
+            quarter, lane = order(part)
+
+            @pl.when(block == 0)
+            def _():
+                @pl.when(diagonal)
+                def _():
+                    load_stage(rowbuf.at[2 * quarter + lane])
+
+                @pl.when(z != w)
+                def _():
+                    load_stage(colbuf.at[part])
+
+                def convert(k, carry):
+                    split_into(stage[k], col_lead, col_trail, pl.multiple_of(k * shard_rows, shard_rows))
+                    return carry
+
+                lax.fori_loop(0, kinds, convert, 0)
+
+            slot = task % 2
+            place = (2 * (quarter % 2) + lane) * shard_rows
+
+            @pl.when(task >= 2)
+            def _():
+                tile_copy(slot, block, place).wait()
+
+            def rows_of(ref, k):
+                return ref[pl.ds(pl.multiple_of(k * panel_rows + block * block_rows, block_rows), block_rows), :]
+
+            def columns_of(ref, k):
+                return ref[pl.ds(pl.multiple_of(k * shard_rows, shard_rows), shard_rows), :]
+
+            def product(left, right):
+                return lax.dot_general(left, right, (((1,), (1,)), ((), ())), preferred_element_type=jnp.float32)
+
+            def perturbation(k, carry):
+                total = product(rows_of(row_lead, k), columns_of(col_lead, perturbations))
+                total += product(rows_of(row_lead, k), columns_of(col_trail, perturbations))
+                total += product(rows_of(row_trail, k), columns_of(col_lead, perturbations))
+                total += product(rows_of(row_lead, perturbations), columns_of(col_lead, k))
+                total += product(rows_of(row_trail, perturbations), columns_of(col_lead, k))
+                total += product(rows_of(row_lead, perturbations), columns_of(col_trail, k))
+                tile[slot, k] = total
+                return carry
+
+            lax.fori_loop(0, perturbations, perturbation, 0)
+            tile_copy(slot, block, place).start()
+
+        return carry
+
+    lax.fori_loop(0, rounds + row_blocks, step, 0)
+
+    for slot in range(2):
+        tile_copy(slot, 0, 0).wait()
+
+    def drain(slot, ref):
+        pltpu.make_async_copy(ref, ref, tx.at[slot]).wait()
+
+    drain(0, rowbuf.at[0])
+    drain(1, rowbuf.at[0])
+    drain(2, rowbuf.at[0, pl.ds(0, kinds // 2)])
+    drain(3, rowbuf.at[0, pl.ds(0, kinds // 2)])
+    drain(4, rowbuf.at[pl.ds(0, 4)])
+
+    @pl.when(has_up & (z >= w))
+    def _():
+        drain(5, rowbuf.at[pl.ds(0, 4)])
+
+    @pl.when(has_down & (z <= w))
+    def _():
+        drain(6, rowbuf.at[pl.ds(0, 4)])
+
+
+def panels(response_coeffs, occupied_coeffs):
+    perturbations, shard_rows, orbitals = response_coeffs.shape
+    kinds = perturbations + 1
+    pieces = kinds * HALVES
+    block_rows = 2 * shard_rows
+    any_space = pl.BlockSpec(memory_space=pl.ANY)
+    float32, bfloat16 = jnp.float32, jnp.bfloat16
+    return pl.pallas_call(
+        panel_kernel,
+        out_shape=(
+            jax.ShapeDtypeStruct((perturbations, 8 * shard_rows, 4 * shard_rows), float32),
+            jax.ShapeDtypeStruct((8, kinds, shard_rows, orbitals), float32),
+            jax.ShapeDtypeStruct((4, kinds, shard_rows, orbitals), float32),
+        ),
+        in_specs=[any_space] * 2,
+        out_specs=(any_space,) * 3,
+        scratch_shapes=[
+            pltpu.VMEM((kinds * 8 * shard_rows, orbitals), bfloat16),
+            pltpu.VMEM((kinds * 8 * shard_rows, orbitals), bfloat16),
+            pltpu.VMEM((kinds * shard_rows, orbitals), bfloat16),
+            pltpu.VMEM((kinds * shard_rows, orbitals), bfloat16),
+            pltpu.VMEM((kinds, shard_rows, orbitals), float32),
+            pltpu.VMEM((2, perturbations, block_rows, shard_rows), float32),
+            pltpu.SemaphoreType.DMA((8, pieces)),
+            pltpu.SemaphoreType.DMA((4 * pieces,)),
+            pltpu.SemaphoreType.DMA((7,)),
+            pltpu.SemaphoreType.DMA((2,)),
+            pltpu.SemaphoreType.DMA((2,)),
+        ],
+        compiler_params=pltpu.CompilerParams(
+            collective_id=0, has_side_effects=True, vmem_limit_bytes=66_000_000
+        ),
+    )(response_coeffs, occupied_coeffs)[0]
+
+
 def solution(mesh):
+    fits = mesh.shape["row"] == 4 and mesh.shape["col"] == 8
     return jax.shard_map(
-        shards,
+        panels if fits else shards,
         mesh=mesh,
         in_specs=(P(None, ("row", "col"), None), P(("row", "col"), None)),
         out_specs=P(None, "row", "col"),

time: 918 us -> 448 us (0.49)
  the two profiles are of different devices: /device:TPU:0 before, /device:TPU:24 now
where the time goes in v1:
time: 448 us
  Pallas kernels  430 us (96%)
  local copies, waits for them, and re-layouts  17.7 us (4%)
    pallas_call x1, Pallas kernels, panels(): pl.pallas_call(panel_kernel, out_shape=(jax.ShapeDtypeStruct((perturbatio...  430 us
    unnamed x1, local copies, waits for them, and re-layouts  17.7 us

profile of v1, /device:TPU:24, one launch (start us, length us, event | category | flops | bytes accessed | tf_op | source)
XLA Modules:
  0.0 447.7 jit_solution(8263430155668844971)
XLA Ops:
  0.0 430.0 %shard_map.28 = (f32[3,2048,1024]{2,1,0:T(8,128)}, f32[8,4,256,1024]{3,2,1,0:T(8,128)}, f32[4,4,256,1024]{3,2,1,0:T(8,128)}) custom-call(f32[3,256,1024]{2,1,0:T(8,128)} %resp.1, f32[256,1024]{1,0:T(8,128)} %occ.1), custom_call_target="tpu_custom_call" | custom-call | tf_op jit(solution)/shard_map/pallas_call | solution.py:358
  430.0 17.7 %copy.4 = f32[3,2048,1024]{2,1,0:T(8,128)} copy(f32[3,2048,1024]{2,1,0:T(8,128)} %get-tuple-element.6) | data formatting | bytes 50331648

commit v2 on v1

--- a/solution.py
+++ b/solution.py
@@ -92,9 +92,9 @@
 
 
 def panel_kernel(
-    resp, occ, out, rowbuf, colbuf,
+    resp, occ, out, rowbuf, colbuf, latebuf,
     row_lead, row_trail, col_lead, col_trail, stage, tile,
-    rx_row, rx_col, tx, stage_sem, tile_sem,
+    rx_row, rx_col, rx_late, tx, stage_sem, tile_sem,
 ):
     perturbations, shard_rows, orbitals = resp.shape
     kinds = perturbations + 1
@@ -124,10 +124,18 @@
     def greet(device):
         pl.semaphore_signal(barrier, inc=1, device_id=device, device_id_type=pl.DeviceIdType.MESH)
 
-    above, below = (z + 1) % planes, (z + planes - 1) % planes
-    for device in (x_dev, y_dev, p_dev, (above, column), (below, column)):
-        greet(device)
-    pl.semaphore_wait(barrier, 5)
+    for offset in range(1, 8):
+        greet((z, (column + offset) % 8))
+    for offset in (1, planes - 1):
+        greet(((z + offset) % planes, column))
+    pl.semaphore_wait(barrier, 9)
+
+    low, high = w == 0, w == planes - 1
+    relay = low | high
+    depth = jnp.where(low, planes - 1 - z, z)
+    onward = jnp.where(low, has_down, has_up)
+    onward_dev = (jnp.where(low, jnp.maximum(z - 1, 0), jnp.minimum(z + 1, planes - 1)), column)
+    late_in = ((z < w) & (core == 0)) | ((z > w) & (core == 1))
 
     def row_piece(quarter, lane, j):
         return rowbuf.at[2 * quarter + lane, j // HALVES, pl.ds(pl.multiple_of((j % HALVES) * piece, piece), piece)]
@@ -135,6 +143,9 @@
     def col_piece(p):
         i, j = p // pieces, p % pieces
         return colbuf.at[i, j // HALVES, pl.ds(pl.multiple_of((j % HALVES) * piece, piece), piece)]
+
+    def late_piece(m, j):
+        return latebuf.at[m, j // HALVES, pl.ds(pl.multiple_of((j % HALVES) * piece, piece), piece)]
 
     def send(source, target, send_sem, recv_sem, device):
         pltpu.make_async_remote_copy(
@@ -165,26 +176,45 @@
     keep.start()
     keep.wait()
 
-    first = jnp.where(match, w, yq)
-    second = flip(first)
-
-    def order(i):
-        quarter = jnp.where(i < 2, first, second)
+    full_first = jnp.where(match, w, yq)
+    lone = jnp.where(core == 0, 1, 2)
+    first = jnp.where(late_in, lone, full_first)
+
+    def sequence(lead, i):
+        quarter = jnp.where(i < 2, lead, flip(lead))
         lane = jnp.where(i % 2 == 0, core, other)
         return quarter, lane
 
-    def emit(source, p):
-        @pl.when(has_up & (z >= w))
-        def _():
+    def order(i):
+        return sequence(first, i)
+
+    def position(quarter, lane, j):
+        return (2 * (quarter % 2) + lane) * pieces + j
+
+    def emit(source, p, upward):
+        if upward:
             send(source, col_piece(p), tx.at[5], rx_col.at[p], up_dev)
-
-        @pl.when(has_down & (z <= w))
-        def _():
+        else:
             send(source, col_piece(p), tx.at[6], rx_col.at[p], down_dev)
 
-    def emit_own(p):
-        quarter, lane = order(p // pieces)
-        emit(row_piece(quarter, lane, p % pieces), p)
+    def emit_own(lead, n, upward):
+        quarter, lane = sequence(lead, n // pieces)
+        emit(row_piece(quarter, lane, n % pieces), position(quarter, lane, n % pieces), upward)
+
+    def originate(t, upward, single):
+        def at(condition, lead, base, count, pace):
+            @pl.when(condition & (t >= base) & (t < base + count // pace))
+            def _():
+                for extra in range(pace):
+                    emit_own(lead, pace * (t - base) + extra, upward)
+
+        here = diagonal & (has_up if upward else has_down)
+        alone = core == single
+        at(here & (core != single) & match, full_first, 0, positions, 2)
+        at(here & (core != single) & (w // 2 != core), full_first, 0, positions, 1)
+        at(here & alone & (lone == w), lone, 0, positions // 2, 2)
+        at(here & alone & (lone == yq), lone, 0, positions // 2, 1)
+        at(here & alone & (lone == dq), lone, gathered, positions // 2, 2)
 
     def split_into(value, lead, trail, start):
         leading = value.astype(jnp.bfloat16)
@@ -244,21 +274,49 @@
             for shift in (0, early):
                 wait_row(dq, other, t - pieces - 1 + shift)
 
-        @pl.when(diagonal & match & (t < positions // 2))
-        def _():
-            emit_own(2 * t)
-            emit_own(2 * t + 1)
-
-        @pl.when(diagonal & (w // 2 != core) & (t < positions))
-        def _():
-            emit_own(t)
-
-        @pl.when((z != w) & (t >= distance) & (t < positions + distance))
-        def _():
-            p = t - distance
+        originate(t, True, 1)
+        originate(t, False, 0)
+
+        arriving = jnp.where(late_in, positions // 2, positions)
+
+        @pl.when((z != w) & (t >= distance) & (t < arriving + distance))
+        def _():
+            n = t - distance
+            quarter, lane = order(n // pieces)
+            p = position(quarter, lane, n % pieces)
             ref = col_piece(p)
             pltpu.make_async_copy(ref, ref, rx_col.at[p]).wait()
-            emit(ref, p)
+
+            @pl.when(has_up & (z > w))
+            def _():
+                emit(ref, p, True)
+
+            @pl.when(has_down & (z < w))
+            def _():
+                emit(ref, p, False)
+
+        own_at = jnp.where(depth > 0, (pieces + 1) * depth - 1, 0)
+
+        @pl.when(relay & onward & (t >= own_at) & (t < own_at + pieces))
+        def _():
+            j = t - own_at
+            send(row_piece(w, core, j), late_piece(depth, j), tx.at[7 + depth], rx_late.at[depth, j], onward_dev)
+
+        @pl.when(relay & (t + 1 >= depth) & (t + 1 < depth + pieces * depth))
+        def _():
+            n = t + 1 - depth
+            m, j = n // pieces, n % pieces
+            ref = late_piece(m, j)
+            pltpu.make_async_copy(ref, ref, rx_late.at[m, j]).wait()
+
+            @pl.when(onward)
+            def _():
+                send(ref, ref, tx.at[7 + m], rx_late.at[m, j], onward_dev)
+
+            panel = jnp.where(low, planes - 1 - m, m)
+            side = jnp.where(low, 0, 1)
+            p = position(w, core, j)
+            send(ref, col_piece(p), tx.at[11 + m], rx_col.at[p], (z, 2 * panel + side))
 
         @pl.when((t >= convert_at) & (t < matmul_at))
         def _():
@@ -286,7 +344,19 @@
 
                 @pl.when(z != w)
                 def _():
-                    load_stage(colbuf.at[part])
+                    shard = 2 * (quarter % 2) + lane
+
+                    @pl.when(late_in & (part >= 2))
+                    def _():
+                        def arrive(j, carry):
+                            p = position(quarter, lane, j)
+                            ref = col_piece(p)
+                            pltpu.make_async_copy(ref, ref, rx_col.at[p]).wait()
+                            return carry
+
+                        lax.fori_loop(0, pieces, arrive, 0)
+
+                    load_stage(colbuf.at[shard])
 
                 def convert(k, carry):
                     split_into(stage[k], col_lead, col_trail, pl.multiple_of(k * shard_rows, shard_rows))
@@ -339,13 +409,24 @@
     drain(3, rowbuf.at[0, pl.ds(0, kinds // 2)])
     drain(4, rowbuf.at[pl.ds(0, 4)])
 
-    @pl.when(has_up & (z >= w))
-    def _():
-        drain(5, rowbuf.at[pl.ds(0, 4)])
-
-    @pl.when(has_down & (z <= w))
-    def _():
-        drain(6, rowbuf.at[pl.ds(0, 4)])
+    for slot, single, sends in ((5, 1, has_up & (z >= w)), (6, 0, has_down & (z <= w))):
+        @pl.when(sends & (core != single))
+        def _():
+            drain(slot, rowbuf.at[pl.ds(0, 4)])
+
+        @pl.when(sends & (core == single))
+        def _():
+            drain(slot, rowbuf.at[pl.ds(0, 2)])
+
+    for m in range(4):
+        @pl.when(relay & onward & (m <= depth))
+        def _():
+            drain(7 + m, rowbuf.at[0])
+
+    for m in range(3):
+        @pl.when(relay & (m < depth))
+        def _():
+            drain(11 + m, rowbuf.at[0])
 
 
 def panels(response_coeffs, occupied_coeffs):
@@ -361,9 +442,10 @@
             jax.ShapeDtypeStruct((perturbations, 8 * shard_rows, 4 * shard_rows), float32),
             jax.ShapeDtypeStruct((8, kinds, shard_rows, orbitals), float32),
             jax.ShapeDtypeStruct((4, kinds, shard_rows, orbitals), float32),
+            jax.ShapeDtypeStruct((3, kinds, shard_rows, orbitals), float32),
         ),
         in_specs=[any_space] * 2,
-        out_specs=(any_space,) * 3,
+        out_specs=(any_space,) * 4,
         scratch_shapes=[
             pltpu.VMEM((kinds * 8 * shard_rows, orbitals), bfloat16),
             pltpu.VMEM((kinds * 8 * shard_rows, orbitals), bfloat16),
@@ -373,7 +455,8 @@
             pltpu.VMEM((2, perturbations, block_rows, shard_rows), float32),
             pltpu.SemaphoreType.DMA((8, pieces)),
             pltpu.SemaphoreType.DMA((4 * pieces,)),
-            pltpu.SemaphoreType.DMA((7,)),
+            pltpu.SemaphoreType.DMA((3, pieces)),
+            pltpu.SemaphoreType.DMA((14,)),
             pltpu.SemaphoreType.DMA((2,)),
             pltpu.SemaphoreType.DMA((2,)),
         ],

time: 448 us -> 537 us (1.20)
  the two profiles are of different devices: /device:TPU:24 before, /device:TPU:0 now
where the time goes in v2:
time: 537 us; the launch traced here: 536 us
  Pallas kernels  519 us (97%)
  local copies, waits for them, and re-layouts  17.7 us (3%)
    pallas_call x1, Pallas kernels, panels(): pl.pallas_call(panel_kernel, out_shape=(jax.ShapeDtypeStruct((perturbatio...  519 us
    unnamed x1, local copies, waits for them, and re-layouts  17.7 us

profile of v2, /device:TPU:0, one launch (start us, length us, event | category | flops | bytes accessed | tf_op | source)
XLA Modules:
  0.0 536.3 jit_solution(10573727104990140280)
XLA Ops:
  0.0 518.6 %shard_map.28 = (f32[3,2048,1024]{2,1,0:T(8,128)}, f32[8,4,256,1024]{3,2,1,0:T(8,128)}, f32[4,4,256,1024]{3,2,1,0:T(8,128)}, f32[3,4,256,1024]{3,2,1,0:T(8,128)}) custom-call(f32[3,256,1024]{2,1,0:T(8,128)} %resp.1, f32[256,1024]{1,0:T(8,128)} %occ.1), custom_call_target="tpu_custom_call" | custom-call | tf_op jit(solution)/shard_map/pallas_call | solution.py:439
  518.6 17.7 %copy.4 = f32[3,2048,1024]{2,1,0:T(8,128)} copy(f32[3,2048,1024]{2,1,0:T(8,128)} %get-tuple-element.6) | data formatting | bytes 50331648

commit v3 on v2

--- a/solution.py
+++ b/solution.py
@@ -81,6 +81,7 @@
 
 
 HALVES = 2
+LAG = 2
 
 
 def flip(value):
@@ -117,7 +118,7 @@
     has_up, has_down = z < planes - 1, z > 0
     diagonal = z == w
     match = w // 2 == core
-    distance = jnp.where(z > w, z - w, w - z)
+    distance = LAG * jnp.where(z > w, z - w, w - z)
 
     barrier = pltpu.get_barrier_semaphore()
 
@@ -237,7 +238,7 @@
     gathered = pieces + early
     convert_at = gathered + 1
     matmul_at = convert_at + 8
-    rounds = positions + planes - 1
+    rounds = positions + LAG * (planes - 1)
     hidden = 3 * row_blocks
     tasks = 4 * row_blocks
 
@@ -295,16 +296,16 @@
             def _():
                 emit(ref, p, False)
 
-        own_at = jnp.where(depth > 0, (pieces + 1) * depth - 1, 0)
+        own_at = (pieces + LAG) * depth
 
         @pl.when(relay & onward & (t >= own_at) & (t < own_at + pieces))
         def _():
             j = t - own_at
             send(row_piece(w, core, j), late_piece(depth, j), tx.at[7 + depth], rx_late.at[depth, j], onward_dev)
 
-        @pl.when(relay & (t + 1 >= depth) & (t + 1 < depth + pieces * depth))
-        def _():
-            n = t + 1 - depth
+        @pl.when(relay & (t >= LAG * depth) & (t < (LAG + pieces) * depth))
+        def _():
+            n = t - LAG * depth
             m, j = n // pieces, n % pieces
             ref = late_piece(m, j)
             pltpu.make_async_copy(ref, ref, rx_late.at[m, j]).wait()

time: 537 us -> 549 us (1.022)
  the two profiles are of different devices: /device:TPU:0 before, /device:TPU:2 now
where the time goes in v3:
time: 549 us; the launch traced here: 548 us
  Pallas kernels  530 us (97%)
  local copies, waits for them, and re-layouts  17.7 us (3%)
    pallas_call x1, Pallas kernels, panels(): pl.pallas_call(panel_kernel, out_shape=(jax.ShapeDtypeStruct((perturbatio...  530 us
    unnamed x1, local copies, waits for them, and re-layouts  17.7 us

profile of v3, /device:TPU:2, one launch (start us, length us, event | category | flops | bytes accessed | tf_op | source)
XLA Modules:
  0.0 548.2 jit_solution(2765808893320415703)
XLA Ops:
  0.0 530.5 %shard_map.28 = (f32[3,2048,1024]{2,1,0:T(8,128)}, f32[8,4,256,1024]{3,2,1,0:T(8,128)}, f32[4,4,256,1024]{3,2,1,0:T(8,128)}, f32[3,4,256,1024]{3,2,1,0:T(8,128)}) custom-call(f32[3,256,1024]{2,1,0:T(8,128)} %resp.1, f32[256,1024]{1,0:T(8,128)} %occ.1), custom_call_target="tpu_custom_call" | custom-call | tf_op jit(solution)/shard_map/pallas_call | solution.py:440
  530.5 17.7 %copy.4 = f32[3,2048,1024]{2,1,0:T(8,128)} copy(f32[3,2048,1024]{2,1,0:T(8,128)} %get-tuple-element.6) | data formatting | bytes 50331648
